TPU v7x, 32 devices: a whole 2x2x4 slice. The times are simulated.
32 devices in a mesh: row: 4 (over x, core), col: 8 (over z, y).
Axes of the slice: x: 2, y: 2, z: 4, core: 2. Of those that a mesh axis runs over, the one named last changes fastest.
Arguments:
- tensor: float32 [1024, 32, 1024], P(None, 'row', 'col'), may hold values from -60 to 60, as said below
- factor_two: float32 [32, 32], P('row'), may hold values from -1 to 1
- factor_three: float32 [32, 32], P('col'), may hold values from -1 to 1
- factor_four: float32 [32, 16], replicated, may hold values from -1 to 1
- factor_init: float32 [1024, 64], replicated, may hold values from -6 to 6
Outputs:
- factor_new: float32 [1024, 64], replicated
- core: float32 [64, 32, 32, 16], P(None, 'row', 'col')
Inputs may be any that keep to these rules, and one draw needn't show every extreme that they name: `tensor`: scales vary from slab to slab.
All inputs are finite; a program needn't handle non-finite values.
Results may differ from a plain program's by a relative error of at most 0.00013.
Values sent between devices are 32-bit elements; how exact they have to be, the bound alone decides.
A program may use at most 128 MiB of HBM per device.

v0:
```python
import jax
import jax.numpy as jnp
from jax import lax
from jax.sharding import PartitionSpec as P


def shards(tensor, factor_two, factor_three, factor_four, factor_init):
    highest = lax.Precision.HIGHEST
    first_len = tensor.shape[0]
    local_two = tensor.shape[1]
    fourth_len = factor_four.shape[0]
    local_three = tensor.shape[2] // fourth_len
    rank_one = factor_init.shape[1]
    data = tensor.reshape(first_len, local_two, local_three, fourth_len)
    fourth = jnp.einsum("abcd,de->abce", data, factor_four, precision=highest)
    whole_two = lax.all_gather(factor_two, "row", axis=0, tiled=True)
    spread_two = lax.all_to_all(fourth, "row", split_axis=0, concat_axis=1, tiled=True)
    projected_two = jnp.einsum("abce,bg->agce", spread_two, whole_two, precision=highest)
    partial_two = lax.all_to_all(projected_two, "row", split_axis=1, concat_axis=0, tiled=True)
    whole_three = lax.all_gather(factor_three, "col", axis=0, tiled=True)
    spread_three = lax.all_to_all(partial_two, "col", split_axis=0, concat_axis=2, tiled=True)
    projected_three = jnp.einsum("agce,cf->agfe", spread_three, whole_three, precision=highest)
    block = lax.all_to_all(projected_three, "col", split_axis=2, concat_axis=0, tiled=True)
    columns = block.reshape(first_len, -1)
    basis = factor_init
    local_gram = jnp.dot(columns, columns.T, precision=highest, preferred_element_type=jnp.float32)
    gram = lax.psum(local_gram, ("row", "col"))
    image = jnp.dot(gram, basis, precision=highest, preferred_element_type=jnp.float32)
    square = jnp.dot(image.T, image, precision=highest, preferred_element_type=jnp.float32)
    lower = jnp.linalg.cholesky(square)
    basis = jax.scipy.linalg.solve_triangular(lower, image.T, lower=True).T
    core = jnp.dot(basis.T, columns, precision=highest, preferred_element_type=jnp.float32)
    return (basis, core.reshape(rank_one, block.shape[1], block.shape[2], block.shape[3]))


def solution(mesh):
    in_specs = (P(None, "row", "col"), P("row", None), P("col", None), P(), P())
    out_specs = (P(), P(None, "row", "col", None))
    return jax.shard_map(shards, mesh=mesh, in_specs=in_specs, out_specs=out_specs, check_vma=False)
```

profile of v0, /device:TPU:0, one launch (start us, length us, event | category | flops | bytes accessed | tf_op | source)
XLA Modules:
  0.0 512.5 jit_solution(1816454857235836736)
XLA Ops:
  7.2 5.5 %copy.18 = f32[1024,8,128]{0,2,1:T(8,128)} copy(f32[1024,8,128]{2,1,0:T(8,128)} %param.5) | data formatting | bytes 8388608 | tf_op args[0]
  12.6 4.2 fusion.12
  16.8 12.2 %copy.19 = f32[1024,8,4,16]{3,2,1,0:T(4,128)} copy(f32[1024,8,4,16]{0,3,2,1:T(8,128)S(1)} %fusion.12) | data formatting | bytes 4194304 | tf_op jit(solution)/shard_map/abcd,de->abce/dot_general | solution.py:15
  29.0 15.5 %reshape.31 = f32[4,1,131072]{2,1,0:T(1,128)} reshape(f32[1024,8,4,16]{3,2,1,0:T(4,128)} %copy.19) | data formatting | bytes 4194304
  44.5 4.4 all-to-all-start
  48.9 26.7 %all_gather.6 = f32[32,32]{1,0:T(8,128)S(1)} all-gather(f32[8,32]{1,0:T(8,128)S(1)} %copy-done.5), channel_id=1, replica_groups=mesh['row'=4,'col'=8] {'row'}, dimensions={0}, use_global_device_ids=true | all-gather | bytes 5120 | tf_op jit(solution)/shard_map/all_gather | solution.py:16
  77.4 7.7 %reduce.6 = f32[4,131072]{1,0:T(4,128)S(1)} reduce(f32[4,1,131072]{2,1,0:T(1,128)} %copy-done.2, f32[]{:T(128)} %broadcast.53), dimensions={1}, to_apply=%all_to_all.50.reduce_sub_computation | reduce | bytes 4194308 | tf_op jit(solution)/shard_map/all_to_all | solution.py:17
  85.1 17.9 %reshape.32 = f32[1024,8,4,16]{3,2,1,0:T(4,128)} reshape(f32[4,131072]{1,0:T(4,128)S(1)} %reduce.6) | data formatting | bytes 4194304
  103.0 12.2 %copy.20 = f32[4,256,8,4,16]{1,2,0,4,3:T(8,128)S(1)} copy(f32[4,256,8,4,16]{4,3,2,1,0:T(4,128)} %bitcast.72) | data formatting | bytes 4194304 | tf_op jit(solution)/shard_map/all_to_all | solution.py:17
  118.4 28.1 %all_to_all.69 = f32[256,32,4,16]{0,3,2,1:T(8,128)S(1)} all-to-all(f32[256,32,4,16]{0,3,2,1:T(8,128)S(1)} %copy.21), channel_id=1, replica_groups=mesh['row'=4,'col'=8] {'row'}, dimensions={1} | all-to-all | bytes 4194304 | tf_op jit(solution)/shard_map/all_to_all | solution.py:19
  146.6 12.1 %copy.37 = f32[256,4,8,4,16]{4,3,2,0,1:T(4,128)} copy(f32[256,4,8,4,16]{0,4,3,2,1:T(8,128)S(1)} %bitcast.78) | data formatting | bytes 4194304 | tf_op jit(solution)/shard_map/all_to_all | solution.py:19
  158.6 15.4 %reshape.33 = f32[8,1,65536]{2,1,0:T(1,128)} reshape(f32[1024,8,4,16]{3,2,1,0:T(4,128)} %bitcast.73) | data formatting | bytes 4194304
  174.0 6.8 %all-to-all-start.2 = ((f32[8,1,65536]{2,1,0:T(1,128)}), f32[8,1,65536]{2,1,0:T(1,128)}, u32[]{:S(2)}, u32[]{:S(2)}) async-start(f32[8,1,65536]{2,1,0:T(1,128)} %reshape.33), calls=%async_computation.2 | async-start | bytes 4194304 | tf_op jit(solution)/shard_map/all_to_all | solution.py:21
  180.9 66.5 %all-gather = f32[8,4,32]{2,1,0:T(4,128)S(1)} all-gather(f32[1,4,32]{2,1,0:T(4,128)S(1)} %bitcast.85), channel_id=1, replica_groups=mesh['row'=4,'col'=8] {'col'}, dimensions={0}, use_global_device_ids=true | all-gather | bytes 4608 | tf_op jit(solution)/shard_map/all_gather | solution.py:20
  247.3 7.2 %reduce.7 = f32[8,65536]{1,0:T(8,128)S(1)} reduce(f32[8,1,65536]{2,1,0:T(1,128)} %all-to-all-done.2, f32[]{:T(128)} %broadcast.53), dimensions={1}, to_apply=%all_to_all.58.reduce_sub_computation | reduce | bytes 4194308 | tf_op jit(solution)/shard_map/all_to_all | solution.py:21
  254.6 17.3 %reshape.34 = f32[1024,8,4,16]{3,2,1,0:T(4,128)} reshape(f32[8,65536]{1,0:T(8,128)S(1)} %reduce.7) | data formatting | bytes 4194304
  271.9 9.8 %copy.35 = f32[8,128,8,4,16]{1,0,4,3,2:T(8,128)S(1)} copy(f32[8,128,8,4,16]{4,3,2,1,0:T(4,128)} %bitcast.74) | data formatting | bytes 4194304 | tf_op jit(solution)/shard_map/all_to_all | solution.py:21
  286.2 46.2 %all_to_all.70 = f32[128,8,32,16]{0,3,1,2:T(8,128)S(1)} all-to-all(f32[128,8,32,16]{0,3,1,2:T(8,128)S(1)} %copy.27), channel_id=1, replica_groups=mesh['row'=4,'col'=8] {'col'}, dimensions={2} | all-to-all | bytes 4194304 | tf_op jit(solution)/shard_map/all_to_all | solution.py:23
  333.7 8.9 %fusion.14 = f32[1024,1024]{1,0:T(8,128)} fusion(f32[64,8,8,128]{3,2,1,0:T(8,128)S(1)} %bitcast.75), kind=kOutput, calls=%fused_computation.20 | convolution fusion | flops 6442450944 | bytes 6291456 | tf_op jit(solution)/shard_map/dot_general | solution.py:26
  344.5 138.8 %all-reduce.2.cloned.1.call-done = f32[1024,1024]{1,0:T(8,128)} async-done(((f32[1024,1024]{1,0:T(8,128)}), f32[1024,1024]{1,0:T(8,128)}) %all-reduce.2.cloned.1.call-update) | async-done | bytes 4194320 | tf_op jit(solution)/shard_map/psum | solution.py:27
  483.4 6.3 %fusion.15 = f32[1024,64]{0,1:T(8,128)S(1)} fusion(f32[1024,1024]{1,0:T(8,128)} %all-reduce.2.cloned.1.call-done, f32[1024,64]{0,1:T(8,128)S(1)} %copy-done), kind=kOutput, calls=%fused_computation.21 | convolution fusion | flops 805306368 | bytes 4718592 | tf_op jit(solution)/shard_map/dot_general | solution.py:28
  490.2 5.8 %cholesky.16 = f32[64,64]{1,0:T(8,128)S(1)} custom-call(f32[64,64]{1,0:T(8,128)S(1)} %fusion.10), custom_call_target="Cholesky" | custom-call | tf_op jit(solution)/shard_map/jit(cholesky)/cholesky | solution.py:30
  497.3 4.9 custom-call.7
  502.7 2.5 fusion.5
  (33 shorter events, 14.9 us)
Async XLA Ops:
  7.2 476.2 %copy-start = (f32[1024,64]{0,1:T(8,128)S(1)}, f32[1024,64]{0,1:T(8,128)}, u32[]{:S(2)}) copy-start(f32[1024,64]{0,1:T(8,128)} %param.9) | copy-start | bytes 786436
  7.2 5.5 %copy-start.4 = (f32[32,16]{0,1:T(8,128)S(1)}, f32[32,16]{0,1:T(8,128)}, u32[]{:S(2)}) copy-start(f32[32,16]{0,1:T(8,128)} %param.8) | copy-start | bytes 6148
  44.5 4.4 copy-start.5
  44.5 31.1 %all-to-all-start = ((f32[4,1,131072]{2,1,0:T(1,128)}), f32[4,1,131072]{2,1,0:T(1,128)S(1)}, u32[]{:S(2)}, u32[]{:S(2)}) async-start(f32[4,1,131072]{2,1,0:T(1,128)} %reshape.31), calls=%async_computation | async-start | bytes 4194304 | tf_op jit(solution)/shard_map/all_to_all | solution.py:17
  75.5 1.4 copy-start.2
  174.0 6.8 %copy-start.6 = (f32[4,32]{1,0:T(4,128)S(1)}, f32[4,32]{1,0:T(4,128)}, u32[]{:S(2)}) copy-start(f32[4,32]{1,0:T(4,128)} %param.7) | copy-start | bytes 1540
  174.0 73.3 %all-to-all-start.2 = ((f32[8,1,65536]{2,1,0:T(1,128)}), f32[8,1,65536]{2,1,0:T(1,128)}, u32[]{:S(2)}, u32[]{:S(2)}) async-start(f32[8,1,65536]{2,1,0:T(1,128)} %reshape.33), calls=%async_computation.2 | async-start | bytes 4194304 | tf_op jit(solution)/shard_map/all_to_all | solution.py:21
  180.8 302.5 %all-reduce.2.cloned.1.call-start = ((), (), s32[]{:S(2)}) async-start(), calls=%async_computation.4 | async-start | bytes 8388608 | tf_op jit(solution)/shard_map/psum | solution.py:27
  344.5 158.2 %copy-start.1 = (f32[64,8,8,128]{3,1,2,0:T(8,128)S(1)}, f32[64,8,8,128]{3,1,2,0:T(8,128)}, u32[]{:S(2)}) copy-start(f32[64,8,8,128]{3,1,2,0:T(8,128)} %copy.41) | copy-start | bytes 6291460
  502.7 2.5 copy-start.3
Sparse Core Ops, SparseCore 0:
  342.8 140.5 all-reduce.1
where the time goes:
time: 518 us; the launch traced here: 512 us
  blocking collectives  168 us (32%)
  waiting for transfers between devices  139 us (27%)
  local copies, waits for them, and re-layouts  127 us (25%)
  other arithmetic  27 us (5%)
  matrix products  26.5 us (5%)
  between operations  14.6 us (3%)
  starting transfers between devices  11.2 us (2%)
    psum x1, waiting for transfers between devices, shards(): gram = lax.psum(local_gram, ('row', 'col'))  139 us
    unnamed x20, local copies, waits for them, and re-layouts  74.8 us
    all_gather x1, blocking collectives, shards(): whole_three = lax.all_gather(factor_three, 'col', axis=0, tiled=True)  66.5 us
    all_to_all x1, blocking collectives, shards(): lax.all_to_all(projected_three, 'col', split_axis=2, concat_axis=0, tiled...  46.2 us
    all_to_all x1, blocking collectives, shards(): lax.all_to_all(projected_two, 'row', split_axis=1, concat_axis=0, tiled=T...  28.1 us
    all_gather x1, blocking collectives, shards(): whole_two = lax.all_gather(factor_two, 'row', axis=0, tiled=True)  26.7 us
    all_to_all x2, local copies, waits for them, and re-layouts, shards(): lax.all_to_all(fourth, 'row', split_axis=0, concat_axis=1, tiled=True)  12.7 us
    dot_general x1, local copies, waits for them, and re-layouts, shards(): fourth = jnp.einsum('abcd,de->abce', data, factor_four, precision=highest)  12.2 us
  transfers between devices with their start and end apart: 3, of which 1 were waited for; matrix products, arithmetic and copies ran while one was open for 0% of the time, Pallas kernels for 0%

commit v1 on v0

--- a/solution.py
+++ b/solution.py
@@ -24,7 +24,7 @@
     columns = block.reshape(first_len, -1)
     basis = factor_init
     local_gram = jnp.dot(columns, columns.T, precision=highest, preferred_element_type=jnp.float32)
-    gram = lax.psum(local_gram, ("row", "col"))
+    gram = lax.psum(lax.psum(local_gram, "col"), "row")
     image = jnp.dot(gram, basis, precision=highest, preferred_element_type=jnp.float32)
     square = jnp.dot(image.T, image, precision=highest, preferred_element_type=jnp.float32)
     lower = jnp.linalg.cholesky(square)

time: 518 us -> 619 us (1.19)
  waiting for transfers between devices: 139 us -> 240 us
    psum x1 -> x2, waiting for transfers between devices: 139 us -> 239 us  [shards(): gram = lax.psum(lax.psum(local_gram, 'col'), 'row')]
  transfers between devices with their start and end apart: 3 -> 4, of which waited for: 1 -> 2; matrix products, arithmetic and copies ran while one was open for 0% -> 0% of each run, Pallas kernels for 0% -> 0%
where the time goes in v1:
time: 619 us; the launch traced here: 613 us
  waiting for transfers between devices  240 us (39%)
  blocking collectives  168 us (27%)
  local copies, waits for them, and re-layouts  127 us (21%)
  other arithmetic  27 us (4%)
  matrix products  26.3 us (4%)
  between operations  14.6 us (2%)
  starting transfers between devices  11.5 us (2%)
    psum x2, waiting for transfers between devices, shards(): gram = lax.psum(lax.psum(local_gram, 'col'), 'row')  239 us
    unnamed x20, local copies, waits for them, and re-layouts  74.8 us
    all_gather x1, blocking collectives, shards(): whole_three = lax.all_gather(factor_three, 'col', axis=0, tiled=True)  66.5 us
    all_to_all x1, blocking collectives, shards(): lax.all_to_all(projected_three, 'col', split_axis=2, concat_axis=0, tiled...  46.2 us
    all_to_all x1, blocking collectives, shards(): lax.all_to_all(projected_two, 'row', split_axis=1, concat_axis=0, tiled=T...  28.1 us
    all_gather x1, blocking collectives, shards(): whole_two = lax.all_gather(factor_two, 'row', axis=0, tiled=True)  26.7 us
    all_to_all x2, local copies, waits for them, and re-layouts, shards(): lax.all_to_all(fourth, 'row', split_axis=0, concat_axis=1, tiled=True)  12.7 us
  transfers between devices with their start and end apart: 4, of which 2 were waited for; matrix products, arithmetic and copies ran while one was open for 0% of the time, Pallas kernels for 0%

profile of v1, /device:TPU:0, one launch (start us, length us, event | category | flops | bytes accessed | tf_op | source)
XLA Modules:
  0.0 613.2 jit_solution(8120457811171776811)
XLA Ops:
  7.2 5.5 copy.18
  12.6 4.2 fusion.12
  16.8 12.2 %copy.19 = f32[1024,8,4,16]{3,2,1,0:T(4,128)} copy(f32[1024,8,4,16]{0,3,2,1:T(8,128)S(1)} %fusion.12) | data formatting | bytes 4194304 | tf_op jit(solution)/shard_map/abcd,de->abce/dot_general | solution.py:15
  29.0 15.5 %reshape.31 = f32[4,1,131072]{2,1,0:T(1,128)} reshape(f32[1024,8,4,16]{3,2,1,0:T(4,128)} %copy.19) | data formatting | bytes 4194304
  44.5 4.4 all-to-all-start
  48.9 26.7 %all_gather.6 = f32[32,32]{1,0:T(8,128)S(1)} all-gather(f32[8,32]{1,0:T(8,128)S(1)} %copy-done.5), channel_id=1, replica_groups=mesh['row'=4,'col'=8] {'row'}, dimensions={0}, use_global_device_ids=true | all-gather | bytes 5120 | tf_op jit(solution)/shard_map/all_gather | solution.py:16
  77.4 7.7 %reduce.6 = f32[4,131072]{1,0:T(4,128)S(1)} reduce(f32[4,1,131072]{2,1,0:T(1,128)} %copy-done.2, f32[]{:T(128)} %broadcast.53), dimensions={1}, to_apply=%all_to_all.50.reduce_sub_computation | reduce | bytes 4194308 | tf_op jit(solution)/shard_map/all_to_all | solution.py:17
  85.1 17.9 %reshape.32 = f32[1024,8,4,16]{3,2,1,0:T(4,128)} reshape(f32[4,131072]{1,0:T(4,128)S(1)} %reduce.6) | data formatting | bytes 4194304
  103.0 12.2 %copy.20 = f32[4,256,8,4,16]{1,2,0,4,3:T(8,128)S(1)} copy(f32[4,256,8,4,16]{4,3,2,1,0:T(4,128)} %bitcast.72) | data formatting | bytes 4194304 | tf_op jit(solution)/shard_map/all_to_all | solution.py:17
  118.4 28.1 %all_to_all.69 = f32[256,32,4,16]{0,3,2,1:T(8,128)S(1)} all-to-all(f32[256,32,4,16]{0,3,2,1:T(8,128)S(1)} %copy.21), channel_id=1, replica_groups=mesh['row'=4,'col'=8] {'row'}, dimensions={1} | all-to-all | bytes 4194304 | tf_op jit(solution)/shard_map/all_to_all | solution.py:19
  146.6 12.1 %copy.37 = f32[256,4,8,4,16]{4,3,2,0,1:T(4,128)} copy(f32[256,4,8,4,16]{0,4,3,2,1:T(8,128)S(1)} %bitcast.78) | data formatting | bytes 4194304 | tf_op jit(solution)/shard_map/all_to_all | solution.py:19
  158.6 15.4 %reshape.33 = f32[8,1,65536]{2,1,0:T(1,128)} reshape(f32[1024,8,4,16]{3,2,1,0:T(4,128)} %bitcast.73) | data formatting | bytes 4194304
  174.0 6.8 %all-to-all-start.2 = ((f32[8,1,65536]{2,1,0:T(1,128)}), f32[8,1,65536]{2,1,0:T(1,128)}, u32[]{:S(2)}, u32[]{:S(2)}) async-start(f32[8,1,65536]{2,1,0:T(1,128)} %reshape.33), calls=%async_computation.2 | async-start | bytes 4194304 | tf_op jit(solution)/shard_map/all_to_all | solution.py:21
  180.9 66.5 %all-gather = f32[8,4,32]{2,1,0:T(4,128)S(1)} all-gather(f32[1,4,32]{2,1,0:T(4,128)S(1)} %bitcast.85), channel_id=1, replica_groups=mesh['row'=4,'col'=8] {'col'}, dimensions={0}, use_global_device_ids=true | all-gather | bytes 4608 | tf_op jit(solution)/shard_map/all_gather | solution.py:20
  247.3 7.2 %reduce.7 = f32[8,65536]{1,0:T(8,128)S(1)} reduce(f32[8,1,65536]{2,1,0:T(1,128)} %all-to-all-done.2, f32[]{:T(128)} %broadcast.53), dimensions={1}, to_apply=%all_to_all.58.reduce_sub_computation | reduce | bytes 4194308 | tf_op jit(solution)/shard_map/all_to_all | solution.py:21
  254.6 17.3 %reshape.34 = f32[1024,8,4,16]{3,2,1,0:T(4,128)} reshape(f32[8,65536]{1,0:T(8,128)S(1)} %reduce.7) | data formatting | bytes 4194304
  271.9 9.8 %copy.35 = f32[8,128,8,4,16]{1,0,4,3,2:T(8,128)S(1)} copy(f32[8,128,8,4,16]{4,3,2,1,0:T(4,128)} %bitcast.74) | data formatting | bytes 4194304 | tf_op jit(solution)/shard_map/all_to_all | solution.py:21
  286.2 46.2 %all_to_all.70 = f32[128,8,32,16]{0,3,1,2:T(8,128)S(1)} all-to-all(f32[128,8,32,16]{0,3,1,2:T(8,128)S(1)} %copy.27), channel_id=1, replica_groups=mesh['row'=4,'col'=8] {'col'}, dimensions={2} | all-to-all | bytes 4194304 | tf_op jit(solution)/shard_map/all_to_all | solution.py:23
  333.7 8.7 %fusion.14 = f32[1024,1024]{1,0:T(8,128)} fusion(f32[64,8,8,128]{3,2,1,0:T(8,128)S(1)} %bitcast.75), kind=kOutput, calls=%fused_computation.20 | convolution fusion | flops 6442450944 | bytes 6291456 | tf_op jit(solution)/shard_map/dot_general | solution.py:26
  342.7 154.5 %all-reduce.3.cloned.1.call-done = f32[1024,1024]{1,0:T(8,128)} async-done(((f32[1024,1024]{1,0:T(8,128)}), f32[1024,1024]{1,0:T(8,128)}) %all-reduce.3.cloned.1.call-update) | async-done | bytes 4194320 | tf_op jit(solution)/shard_map/psum | solution.py:27
  499.1 85.0 %all-reduce.5.cloned.1.call-done = f32[1024,1024]{1,0:T(8,128)} async-done(((f32[1024,1024]{1,0:T(8,128)}), f32[1024,1024]{1,0:T(8,128)}) %all-reduce.5.cloned.1.call-update) | async-done | bytes 4194320 | tf_op jit(solution)/shard_map/psum | solution.py:27
  584.1 6.3 %fusion.15 = f32[1024,64]{0,1:T(8,128)S(1)} fusion(f32[1024,1024]{1,0:T(8,128)} %all-reduce.5.cloned.1.call-done, f32[1024,64]{0,1:T(8,128)S(1)} %copy-done), kind=kOutput, calls=%fused_computation.21 | convolution fusion | flops 805306368 | bytes 4718592 | tf_op jit(solution)/shard_map/dot_general | solution.py:28
  590.9 5.8 cholesky.16
  598.1 4.9 custom-call.7
  (36 shorter events, 17.7 us)
Async XLA Ops:
  7.2 576.9 %copy-start = (f32[1024,64]{0,1:T(8,128)S(1)}, f32[1024,64]{0,1:T(8,128)}, u32[]{:S(2)}) copy-start(f32[1024,64]{0,1:T(8,128)} %param.9) | copy-start | bytes 786436
  7.2 5.5 copy-start.4
  44.5 4.4 copy-start.5
  44.5 31.1 %all-to-all-start = ((f32[4,1,131072]{2,1,0:T(1,128)}), f32[4,1,131072]{2,1,0:T(1,128)S(1)}, u32[]{:S(2)}, u32[]{:S(2)}) async-start(f32[4,1,131072]{2,1,0:T(1,128)} %reshape.31), calls=%async_computation | async-start | bytes 4194304 | tf_op jit(solution)/shard_map/all_to_all | solution.py:17
  75.5 1.4 copy-start.2
  174.0 6.8 %copy-start.6 = (f32[4,32]{1,0:T(4,128)S(1)}, f32[4,32]{1,0:T(4,128)}, u32[]{:S(2)}) copy-start(f32[4,32]{1,0:T(4,128)} %param.7) | copy-start | bytes 1540
  174.0 73.3 %all-to-all-start.2 = ((f32[8,1,65536]{2,1,0:T(1,128)}), f32[8,1,65536]{2,1,0:T(1,128)}, u32[]{:S(2)}, u32[]{:S(2)}) async-start(f32[8,1,65536]{2,1,0:T(1,128)} %reshape.33), calls=%async_computation.2 | async-start | bytes 4194304 | tf_op jit(solution)/shard_map/all_to_all | solution.py:21
  180.8 316.4 %all-reduce.3.cloned.1.call-start = ((), (), s32[]{:S(2)}) async-start(), calls=%async_computation.4 | async-start | bytes 8388608 | tf_op jit(solution)/shard_map/psum | solution.py:27
  342.4 241.7 %all-reduce.5.cloned.1.call-start = ((), (), s32[]{:S(2)}) async-start(), calls=%async_computation.5 | async-start | bytes 8388608 | tf_op jit(solution)/shard_map/psum | solution.py:27
  499.1 104.3 %copy-start.1 = (f32[64,8,8,128]{3,1,2,0:T(8,128)S(1)}, f32[64,8,8,128]{3,1,2,0:T(8,128)}, u32[]{:S(2)}) copy-start(f32[64,8,8,128]{3,1,2,0:T(8,128)} %copy.41) | copy-start | bytes 6291460
  603.4 2.5 copy-start.3
Sparse Core Ops, SparseCore 0:
  342.6 154.6 all-reduce.2
  499.6 84.4 all-reduce.4
